TPU v7x, 256 devices: a whole 4x4x8 slice. The times are simulated.
256 devices in a mesh: tm: 2 (over z_lo), chan: 32 (over y, x, core), bl: 4 (over z_hi).
Axes of the slice: x: 4, y: 4, z: 8 (z_hi: 4, z_lo: 2; z = z_hi * 2 + z_lo), core: 2. Of those that a mesh axis runs over, the one named last changes fastest.
Arguments:
- voltages: bfloat16 [2, 256, 1024, 512], P(None, ('chan', 'bl'), None, 'tm'), may hold values from -6 to 6
Outputs:
- visibilities: bfloat16 [2, 1024, 4, 256, 256], P(None, ('chan', 'bl'), 'tm')
All inputs are finite; a program needn't handle non-finite values.
Results may differ from a plain program's by a relative error of at most 0.0051.
Values may be sent and summed in bfloat16 or wider, within the bound.
A program may use at most 64 MiB of HBM per device.

v0:
```python
import jax
import jax.numpy as jnp
from jax import lax
from jax.sharding import PartitionSpec as P

HALF = 128


def in_blocks(x, dim, count):
    before, after = (x.shape[:dim], x.shape[dim + 1 :])
    return jnp.moveaxis(x.reshape(*before, count, -1, *after), dim, 0)


def laid_out(parts, dim):
    parts = jnp.moveaxis(parts, 0, dim)
    shape = parts.shape
    return parts.reshape(*shape[:dim], shape[dim] * shape[dim + 1], *shape[dim + 2 :])


def one_exchange(x, axis, axes, splits, concats):
    sizes = [lax.axis_size(a) for a in axes]
    parts = in_blocks(x, splits[0], sizes[0])
    parts = jnp.moveaxis(in_blocks(parts, splits[1] + 1, sizes[1]), 0, 1)
    inside = parts.shape[2:]
    parts = parts.reshape(-1, *inside)
    parts = lax.all_to_all(parts, axis, split_axis=0, concat_axis=0, tiled=True)
    parts = laid_out(parts.reshape(*sizes, *inside), concats[0] + 1)
    return laid_out(parts, concats[1])


def passed_along(block, axis, distance):
    devices = range(lax.axis_size(axis))
    route = [(i - distance, i) for i in devices if i - distance in devices]
    return lax.ppermute(block, axis, route)


def tapers(length):
    steps = jnp.arange(length, dtype=jnp.float32)
    taper_early = jnp.sin(jnp.pi * (steps + 0.5) / (2.0 * length))
    taper_late = jnp.sin(jnp.pi * (steps + 0.5 + length) / (2.0 * length))
    return (taper_early, taper_late)


def weighted(block, taper):
    return (block.astype(jnp.float32) * taper).astype(jnp.bfloat16)


def products(stacked):
    signals = stacked.shape[0] // 2
    gram = jnp.einsum("pct,qct->cpq", stacked, stacked, preferred_element_type=jnp.float32)
    real_part = gram[:, :signals, :signals] + gram[:, signals:, signals:]
    imag_part = gram[:, signals:, :signals] - gram[:, :signals, signals:]
    return (real_part, imag_part)


def local(voltages):
    turned = one_exchange(voltages, ("chan", "bl"), ("chan", "bl"), (2, 2), (1, 1))
    groups_bl = lax.axis_size("bl")
    groups_chan = lax.axis_size("chan")
    per_device = turned.shape[1] // (groups_bl * groups_chan)
    shaped = turned.reshape(2, groups_bl, groups_chan, per_device, turned.shape[2], turned.shape[3])
    turned = shaped.transpose(0, 2, 1, 3, 4, 5).reshape(turned.shape)
    signals = turned.shape[1]
    channels = turned.shape[2]
    samples = turned.shape[3]
    halves = samples // HALF
    scale = 1.0 / HALF
    taper_early, taper_late = tapers(HALF)
    stacked = turned.reshape(2 * signals, channels, samples)
    lates = []
    earlies = []
    for index in range(halves):
        piece = stacked[:, :, index * HALF : (index + 1) * HALF]
        lates.append(products(weighted(piece, taper_late)))
        if index + 1 < halves:
            earlies.append(products(weighted(piece, taper_early)))
    tail = turned[:, :, :, samples - HALF :]
    received = passed_along(tail, "tm", 1)
    previous = products(weighted(received.reshape(2 * signals, channels, HALF), taper_early))
    real_list = []
    imag_list = []
    for index in range(halves):
        late_real, late_imag = lates[index]
        real_list.append(((late_real + previous[0]) * scale).astype(jnp.bfloat16))
        imag_list.append(((late_imag + previous[1]) * scale).astype(jnp.bfloat16))
        if index + 1 < halves:
            previous = earlies[index]
    return jnp.stack([jnp.stack(real_list, 1), jnp.stack(imag_list, 1)], 0)


def solution(mesh):
    return jax.shard_map(
        local,
        mesh=mesh,
        in_specs=(P(None, ("chan", "bl"), None, "tm"),),
        out_specs=P(None, ("chan", "bl"), "tm", None, None),
        check_vma=False,
    )
```

profile of v0, /device:TPU:64, one launch (start us, length us, event | category | flops | bytes accessed | tf_op | source)
XLA Modules:
  0.0 109.6 jit_solution(16235756983169589690)
XLA Ops:
  0.0 1.7 %fusion.27 = (bf16[32,2,2,8,256]{4,3,0,2,1:T(8,128)(2,1)S(1)}, bf16[32,2,2,8,256]{4,3,0,2,1:T(8,128)(2,1)S(1)}, bf16[32,2,2,8,256]{4,3,0,2,1:T(8,128)(2,1)S(1)}, bf16[32,2,2,8,256]{4,3,0,2,1:T(8,128)(2,1)S(1)}) fusion(bf16[32,2,2,32,256]{4,3,0,2,1:T(8,128)(2,1)} %bitcast.42), kind=kLoop, calls=%fused_computation.45 | loop fusion | bytes 4194304 | tf_op jit(solution)/shard_map/slice
  1.7 0.3 pad_maximum_fusion.1
  2.0 0.2 copy.6
  2.3 67.6 %all_to_all.5 = bf16[128,2,2,8,256]{4,3,2,1,0:T(8,128)(2,1)S(1)} all-to-all(bf16[128,2,2,8,256]{4,3,2,1,0:T(8,128)(2,1)S(1)} %bitcast.40), channel_id=1, replica_groups=mesh['tm'=2,'chan'=32,'bl'=4] {'chan','bl'}, dimensions={0} | all-to-all | bytes 4194304 | tf_op jit(solution)/shard_map/all_to_all | solution.py:26
  69.9 0.3 copy.9
  70.2 0.1 slice.99
  70.2 3.6 %collective-permute-start = (bf16[2,256,8,128]{3,2,1,0:T(8,128)(2,1)S(1)}, bf16[2,256,8,128]{3,2,1,0:T(8,128)(2,1)S(1)}, u32[]{:S(2)}, u32[]{:S(2)}) collective-permute-start(bf16[2,256,8,128]{3,2,1,0:T(8,128)(2,1)S(1)} %slice.99), channel_id=1, source_target_pairs={{0,128},{1,129},{2,130},{3,131},{4,132},{5,133},{6,134},{7,135},{8... | collective-permute-start | bytes 3145736 | tf_op jit(solution)/shard_map/ppermute | solution.py:34
  73.9 0.1 multiply_sine_fusion
  73.9 22.3 %collective-permute-done = bf16[2,256,8,128]{3,2,1,0:T(8,128)(2,1)S(1)} collective-permute-done((bf16[2,256,8,128]{3,2,1,0:T(8,128)(2,1)S(1)}, bf16[2,256,8,128]{3,2,1,0:T(8,128)(2,1)S(1)}, u32[]{:S(2)}, u32[]{:S(2)}) %collective-permute-start) | collective-permute-done | bytes 1048608 | tf_op jit(solution)/shard_map/ppermute | solution.py:34
  96.2 0.8 fusion
  97.0 1.3 %fusion.23 = f32[8,512,512]{2,1,0:T(8,128)S(1)} fusion(bf16[512,8,128]{2,1,0:T(8,128)(2,1)S(1)} %get-tuple-element.16), kind=kOutput, calls=%fused_computation.39 | convolution fusion | flops 536870912 | bytes 9437184 | tf_op jit(solution)/shard_map/pct,qct->cpq/dot_general | solution.py:50
  98.3 1.3 %fusion.25 = f32[8,512,512]{2,1,0:T(8,128)S(1)} fusion(bf16[512,8,128]{2,1,0:T(8,128)(2,1)S(1)} %get-tuple-element.9), kind=kOutput, calls=%fused_computation.41 | convolution fusion | flops 536870912 | bytes 9437184 | tf_op jit(solution)/shard_map/pct,qct->cpq/dot_general | solution.py:50
  99.6 1.3 %fusion.19 = f32[8,512,512]{2,1,0:T(8,128)S(1)} fusion(bf16[512,8,128]{2,1,0:T(8,128)(2,1)S(1)} %get-tuple-element.11), kind=kOutput, calls=%fused_computation.35 | convolution fusion | flops 536870912 | bytes 9437184 | tf_op jit(solution)/shard_map/pct,qct->cpq/dot_general | solution.py:50
  100.8 1.3 %fusion.21 = f32[8,512,512]{2,1,0:T(8,128)S(1)} fusion(bf16[512,8,128]{2,1,0:T(8,128)(2,1)S(1)} %get-tuple-element.10), kind=kOutput, calls=%fused_computation.37 | convolution fusion | flops 536870912 | bytes 9437184 | tf_op jit(solution)/shard_map/pct,qct->cpq/dot_general | solution.py:50
  102.1 2.2 %fusion.15 = (bf16[8,1,256,256]{3,2,0,1:T(8,128)(2,1)S(1)}, bf16[8,1,256,256]{3,2,0,1:T(8,128)(2,1)S(1)}) fusion(f32[8,512,512]{2,1,0:T(8,128)S(1)} %fusion.23, f32[8,512,512]{2,1,0:T(8,128)S(1)} %fusion.25), kind=kLoop, calls=%fused_computation.31 | loop fusion | flops 5242880 | bytes 18874368 | tf_op jit(solution)/shard_map/stack | solution.py:88
  104.3 2.2 %fusion.16 = (bf16[8,1,256,256]{3,2,0,1:T(8,128)(2,1)S(1)}, bf16[8,1,256,256]{3,2,0,1:T(8,128)(2,1)S(1)}) fusion(f32[8,512,512]{2,1,0:T(8,128)S(1)} %fusion.19, f32[8,512,512]{2,1,0:T(8,128)S(1)} %fusion.21), kind=kLoop, calls=%fused_computation.32 | loop fusion | flops 5242880 | bytes 18874368 | tf_op jit(solution)/shard_map/stack | solution.py:88
  106.5 0.2 maximum_bitcast_fusion
  106.7 0.2 maximum_bitcast_fusion.1
  106.9 0.4 pad_maximum_fusion
  107.3 2.3 %copy.19 = bf16[2,8,2,256,256]{4,3,2,1,0:T(8,128)(2,1)} copy(bf16[2,8,2,256,256]{4,3,1,2,0:T(8,128)(2,1)S(1)} %pad_maximum_fusion) | data formatting | bytes 8388608 | tf_op jit(solution)/shard_map/stack | solution.py:88
Async XLA Ops:
  70.2 26.0 %collective-permute-start = (bf16[2,256,8,128]{3,2,1,0:T(8,128)(2,1)S(1)}, bf16[2,256,8,128]{3,2,1,0:T(8,128)(2,1)S(1)}, u32[]{:S(2)}, u32[]{:S(2)}) collective-permute-start(bf16[2,256,8,128]{3,2,1,0:T(8,128)(2,1)S(1)} %slice.99), channel_id=1, source_target_pairs={{0,128},{1,129},{2,130},{3,131},{4,132},{5,133},{6,134},{7,135},{8... | collective-permute-start | bytes 3145736 | tf_op jit(solution)/shard_map/ppermute | solution.py:34
where the time goes:
time: 111 us; the launch traced here: 110 us
  blocking collectives  67.6 us (61%)
  waiting for transfers between devices  22.3 us (20%)
  other arithmetic  6.32 us (6%)
  matrix products  5.05 us (5%)
  local copies, waits for them, and re-layouts  4.63 us (4%)
  starting transfers between devices  3.6 us (3%)
    all_to_all x1, blocking collectives, one_exchange(): parts = lax.all_to_all(parts, axis, split_axis=0, concat_axis=0, tiled=True)  67.6 us
    ppermute x1, waiting for transfers between devices, passed_along(): return lax.ppermute(block, axis, route)  22.3 us
    another operation x5, other arithmetic, local(): return jnp.stack([jnp.stack(real_list, 1), jnp.stack(imag_list, 1)], 0)  5.19 us
    dot_general x4, matrix products, products(): jnp.einsum('pct,qct->cpq', stacked, stacked, preferred_element_type=jnp.f...  5.05 us
    ppermute x1, starting transfers between devices, passed_along(): return lax.ppermute(block, axis, route)  3.6 us
    another operation x1, local copies, waits for them, and re-layouts, local(): return jnp.stack([jnp.stack(real_list, 1), jnp.stack(imag_list, 1)], 0)  2.29 us
  transfers between devices with their start and end apart: 1, of which 1 were waited for; matrix products, arithmetic and copies ran while one was open for 0% of the time, Pallas kernels for 0%

commit v1 on v0

v1 whole, which is shorter than its diff:
```python
import jax, jax.numpy as jnp, functools
from jax import lax
from jax.sharding import PartitionSpec as P
from jax.experimental import pallas as pl
from jax.experimental.pallas import tpu as pltpu
MESH = pl.DeviceIdType.MESH
FL = dict(relay=True, order=(3, 1, 2, 0), lag=4, xy=True)

def comm_kernel(fl, v, out, s, g, rxy, rz, sx, sz, sr, fin):
    t, c, b = lax.axis_index("tm"), lax.axis_index("chan"), lax.axis_index("bl")
    y, l = lax.div(c, 8), lax.rem(c, 8)

    def piece(cc, bb, half):
        return v.at[:, :, cc * 4 + bb, :, pl.ds(half * 128, 128)]

    def spot(o, half, cc):
        return g.at[half, b, cc] if o == 0 else s.at[o - 1, half, cc]

    sem = pltpu.get_barrier_semaphore()
    def greet(**k):
        pl.semaphore_signal(sem, inc=1, device_id=k, device_id_type=MESH)
    for o in (2, 1, 3):
        greet(bl=lax.rem(b + o, 4))
    greet(tm=1 - t)
    far = jnp.where(t == 0, 1, -1)
    greet(tm=1 - t, bl=lax.rem(b - 2 * far + 8, 4))
    greet(tm=1 - t, bl=lax.rem(b - far + 8, 4))
    def greet_xy(i, _):
        greet(chan=lax.rem(c + i, 32))
        return 0
    lax.fori_loop(1, 32, greet_xy, 0)
    for half in (1, 0):
        for o in (2, 3, 1, 0):
            pltpu.make_async_copy(piece(c, lax.rem(b + o, 4), half), spot(o, half, c), rxy.at[o, half, y]).start()
    pl.semaphore_wait(sem, 37)
    if not fl["xy"]:
        for half in (1, 0):
            for o in range(4):
                pltpu.make_async_copy(piece(c, lax.rem(b + o, 4), half), spot(o, half, c), rxy.at[o, half, y]).wait()

    def xysend(half, o, d):
        def send(j, _):
            cc = lax.rem(y + d, 4) * 8 + lax.rem(l + j, 8)
            pltpu.make_async_remote_copy(
                src_ref=piece(cc, lax.rem(b + o, 4), half), dst_ref=spot(o, half, c),
                send_sem=sx.at[o, half], recv_sem=rxy.at[o, half, y],
                device_id={"chan": cc}, device_id_type=MESH).start()
            return 0
        lax.fori_loop(1 if d == 0 else 0, 8, send, 0)

    def rows(ref):
        return ref
    def arrived(ref, sm):
        pltpu.make_async_copy(ref, ref, sm).wait()

    def yg(d):
        return lax.rem(y + 4 - d, 4)
    def eight(d):
        return pl.ds(pl.multiple_of(yg(d) * 8, 8), 8)

    def zsend(half, o, d):
        part = s.at[o - 1, half, eight(d)]
        if fl["xy"]: arrived(part, rxy.at[o, half, yg(d)])
        if half == 1 and o != 1 and fl["relay"]:
            to_t = jnp.int32(1)
            h = jnp.where(t == 0, 2, 1)
        else:
            to_t, h = t, half
        pltpu.make_async_remote_copy(
            src_ref=part, dst_ref=g.at[h, b, eight(d)],
            send_sem=sz.at[o, half], recv_sem=rz.at[h, o, yg(d)],
            device_id={"bl": lax.rem(b + o, 4), "tm": to_t}, device_id_type=MESH).start()

    def relay(d, o, h_from, h_to):
        src = lax.rem(b + 4 - o, 4)
        pltpu.make_async_remote_copy(
            src_ref=g.at[h_from, src, eight(d)], dst_ref=g.at[h_to, src, eight(d)],
            send_sem=sr.at[o], recv_sem=rz.at[h_to, o, yg(d)],
            device_id={"tm": 1 - t}, device_id_type=MESH).start()

    def landed(h, o, d):
        arrived(g.at[h, lax.rem(b + 4 - o, 4), eight(d)], rz.at[h, o, yg(d)])

    order = fl["order"]
    units = [(half, o, d) for half in (1, 0) for d in range(4) for o in order]
    lag = fl["lag"]
    done = [0]
    def advance(k):
        while done[0] < min(k, len(units)):
            if fl["xy"]: xysend(*units[done[0]])
            done[0] += 1
    def relays(d):
        @pl.when(t == 0)
        def _():
            landed(1, 1, d)
            relay(d, 1, 1, 2)
        @pl.when(t == 1)
        def _():
            for o in (2, 3):
                landed(2, o, d)
                relay(d, o, 2, 1)
    for n, u in enumerate(units):
        advance(n + 1 + lag)
        half, o, d = u
        if half == 0 and n % 4 == 0 and fl["relay"]:
            relays(d)
        if o > 0:
            zsend(half, o, d)
        elif half == 1:
            if fl["xy"]: arrived(g.at[1, b, eight(d)], rxy.at[0, 1, yg(d)])
            if fl["relay"]:
                @pl.when(t == 0)
                def _():
                    relay(d, 0, 1, 2)

    if fl['relay']:
        @pl.when(t == 0)
        def _():
            for o in (2, 3):
                for d in range(4):
                    landed(1, o, d)

        @pl.when(t == 1)
        def _():
            for o in (0, 1):
                for d in range(4):
                    landed(2, o, d)
            for o in (2, 3, 1):
                for d in range(4):
                    landed(1, o, d)
    else:
        for o in (2,3,1):
            for d in range(4):
                landed(1, o, d)
    for d in range(4):
        if fl["xy"]: arrived(g.at[0, b, eight(d)], rxy.at[0, 0, yg(d)])
    for o in (2, 3, 1):
        for d in range(4):
            landed(0, o, d)
    for o in range(4):
        for half in range(2):
            if fl["xy"]: arrived(s.at[0, 0, pl.ds(0, 31)], sx.at[o, half])
            if o > 0:
                arrived(s.at[0, 0], sz.at[o, half])
    if fl['relay']:
        @pl.when(t == 0)
        def _():
            for o in (0, 1):
                arrived(s.at[0, 0], sr.at[o])
        @pl.when(t == 1)
        def _():
            for o in (2, 3):
                arrived(s.at[0, 0], sr.at[o])
    cp = pltpu.make_async_copy(g, out, fin)
    cp.start()
    cp.wait()


def comm(v):
    bf = jnp.bfloat16
    D = pltpu.SemaphoreType.DMA
    return pl.pallas_call(
        functools.partial(comm_kernel, dict(FL)),
        out_shape=jax.ShapeDtypeStruct((3, 4, 32, 2, 2, 8, 128), bf),
        in_specs=[pl.BlockSpec(memory_space=pl.ANY)],
        out_specs=pl.BlockSpec(memory_space=pl.ANY),
        scratch_shapes=[
            pltpu.VMEM((3, 2, 32, 2, 2, 8, 128), bf),
            pltpu.VMEM((3, 4, 32, 2, 2, 8, 128), bf),
            D((4, 2, 4)), D((3, 4, 4)), D((4, 2)), D((4, 2)), D((4,)), D,
        ],
        compiler_params=pltpu.CompilerParams(collective_id=0, has_side_effects=True),
    )(v)


HALF = 128


def tapers(length):
    steps = jnp.arange(length, dtype=jnp.float32)
    taper_early = jnp.sin(jnp.pi * (steps + 0.5) / (2.0 * length))
    taper_late = jnp.sin(jnp.pi * (steps + 0.5 + length) / (2.0 * length))
    return (taper_early, taper_late)


def weighted(block, taper):
    return (block.astype(jnp.float32) * taper).astype(jnp.bfloat16)


def local(voltages):
    g = comm(voltages.reshape(2, 2, 128, 8, 256))
    t = lax.axis_index("tm")
    x = g.transpose(0, 5, 3, 2, 1, 4, 6).reshape(3, 8, 2, 256, 128)
    early, late = tapers(HALF)
    zero = jnp.zeros((), jnp.bfloat16)
    tail = jnp.where(t == 1, weighted(x[2], early), zero)
    l0, l1, e0 = weighted(x[0], late), weighted(x[1], late), weighted(x[0], early)
    def win(lo, ea):
        a = jnp.concatenate([lo[:, 0], lo[:, 1], ea[:, 0], ea[:, 1]], -1)
        m = jnp.concatenate([lo[:, 1], -lo[:, 0], ea[:, 1], -ea[:, 0]], -1)
        re = jnp.einsum("cpk,cqk->cpq", a, a, preferred_element_type=jnp.float32)
        im = jnp.einsum("cpk,cqk->cpq", m, a, preferred_element_type=jnp.float32)
        return jnp.stack([re, im], 0) * (1.0 / HALF)
    return jnp.stack([win(l0, tail), win(l1, e0)], 2).astype(jnp.bfloat16)


def solution(mesh):
    return jax.shard_map(
        local,
        mesh=mesh,
        in_specs=(P(None, ("chan", "bl"), None, "tm"),),
        out_specs=P(None, ("chan", "bl"), "tm", None, None),
        check_vma=False,
    )
```

time: 111 us -> 94.6 us (0.85)
  the two profiles are of different devices: /device:TPU:64 before, /device:TPU:33 now
where the time goes in v1:
time: 94.6 us
  Pallas kernels  79.5 us (84%)
  other arithmetic  5.93 us (6%)
  matrix products  5.5 us (6%)
  local copies, waits for them, and re-layouts  3.47 us (4%)
    pallas_call x1, Pallas kernels, comm(): pl.pallas_call(functools.partial(comm_kernel, dict(FL)), out_shape=jax.Sh...  79.5 us
    convert_element_type x2, other arithmetic, weighted(): return (block.astype(jnp.float32) * taper).astype(jnp.bfloat16)  3.71 us
    dot_general x2, matrix products, win(): im = jnp.einsum('cpk,cqk->cpq', m, a, preferred_element_type=jnp.float32)  2.75 us
    dot_general x2, matrix products, win(): re = jnp.einsum('cpk,cqk->cpq', a, a, preferred_element_type=jnp.float32)  2.75 us
    another operation x1, local copies, waits for them, and re-layouts, local(): return jnp.stack([win(l0, tail), win(l1, e0)], 2).astype(jnp.bfloat16)  2.29 us

profile of v1, /device:TPU:33, one launch (start us, length us, event | category | flops | bytes accessed | tf_op | source)
XLA Modules:
  0.0 94.6 jit_solution(2282956306598207169)
XLA Ops:
  0.1 79.5 %shard_map.17 = bf16[3,4,32,2,2,8,128]{6,5,4,3,2,1,0:T(8,128)(2,1)} custom-call(bf16[2,2,128,8,256]{4,3,2,1,0:T(8,128)(2,1)} %bitcast.41), custom_call_target="tpu_custom_call" | custom-call | tf_op jit(solution)/shard_map/pallas_call | solution.py:162
  79.6 2.7 %slice_convert_fusion.1 = (f32[1,8,2,32,4,2,128]{6,1,5,2,3,4,0:T(8,128)S(1)}, f32[1,8,2,32,4,2,128]{6,1,5,2,3,4,0:T(8,128)S(1)}, f32[1,8,2,32,4,2,128]{6,1,5,2,3,4,0:T(8,128)S(1)}) fusion(bf16[3,8,2,32,4,2,128]{6,1,5,2,3,4,0:T(8,128)(2,1)} %bitcast.37), kind=kLoop, calls=%fused_computation.35 | loop fusion | flops 1572864 | bytes 9437184 | tf_op jit(solution)/shard_map/convert_element_type | solution.py:187
  82.3 0.2 copy.5
  82.6 0.5 fusion.26
  83.1 0.1 fusion.32
  83.2 0.3 copy.7
  83.5 0.3 copy.3
  83.8 1.0 %multiply_convert_fusion.1 = (bf16[8,2,256,128]{3,2,0,1:T(8,128)(2,1)S(1)}, bf16[8,2,256,128]{3,2,0,1:T(8,128)(2,1)S(1)}, bf16[8,2,256,128]{3,2,0,1:T(8,128)(2,1)S(1)}) fusion(f32[8,2,256,128]{3,0,2,1:T(8,128)S(1)} %bitcast.40, f32[128]{0:T(128)S(1)} %multiply_sine_fusion.1, f32[128]{0:T(128)S(1)} %multiply_sine_fusion, f32[8,2,256,128]{3,0,2,1:T(8,128)S(1)} %bitcast.39), kind=kLoop, calls=%fused_computation.28 | loop fusion | flops 3145728 | bytes 7341056 | tf_op jit(solution)/shard_map/convert_element_type | solution.py:187
  84.8 0.1 fusion.34
  84.8 0.2 slice_bitcast_fusion.1
  85.0 0.1 fusion.31
  85.2 0.2 slice_bitcast_fusion.5
  85.3 1.4 %fusion.23 = f32[1,8,1,256,256]{4,3,1,2,0:T(8,128)S(1)} fusion(bf16[8,256,128]{2,1,0:T(8,128)(2,1)S(1)} %fusion.32, bf16[8,256,128]{2,1,0:T(8,128)(2,1)S(1)} %get-tuple-element.13, bf16[8,256,128]{2,1,0:T(8,128)(2,1)S(1)} %get-tuple-element.21, bf16[8,256,128]{2,1,0:T(8,128)(2,1)S(1)} %get-tuple-element.23, bf16[8,256,128]{2,1,0:T(8,128)(2,1)S(1)} %get-tuple-element.12, ...), kind=kOutput, calls=%fused_computation.30 | convolution fusion | flops 553648128 | bytes 5242880 | tf_op jit(solution)/shard_map/cpk,cqk->cpq/dot_general | solution.py:202
  86.7 1.4 %convolution_bitcast_fusion.1 = f32[1,8,1,256,256]{4,3,1,2,0:T(8,128)S(1)} fusion(bf16[8,256,128]{2,1,0:T(8,128)(2,1)S(1)} %get-tuple-element.13, bf16[8,256,128]{2,1,0:T(8,128)(2,1)S(1)} %get-tuple-element.12, bf16[8,256,128]{2,1,0:T(8,128)(2,1)S(1)} %get-tuple-element.23, bf16[8,256,128]{2,1,0:T(8,128)(2,1)S(1)} %get-tuple-element.24), kind=kOutput, calls=%fused_computation.32 | convolution fusion | flops 545259520 | bytes 4194304 | tf_op jit(solution)/shard_map/cpk,cqk->cpq/dot_general | solution.py:201
  88.1 0.5 fusion
  88.6 1.4 %fusion.20 = f32[1,8,1,256,256]{4,3,1,2,0:T(8,128)S(1)} fusion(bf16[8,256,128]{2,1,0:T(8,128)(2,1)S(1)} %fusion.34, bf16[8,256,128]{2,1,0:T(8,128)(2,1)S(1)} %get-tuple-element.17, bf16[8,256,128]{2,1,0:T(8,128)(2,1)S(1)} %get-tuple-element.22, bf16[8,256,128]{2,1,0:T(8,128)(2,1)S(1)} %get-tuple-element.19, bf16[8,256,128]{2,1,0:T(8,128)(2,1)S(1)} %get-tuple-element.16, ...), kind=kOutput, calls=%fused_computation.29 | convolution fusion | flops 553648128 | bytes 5242880 | tf_op jit(solution)/shard_map/cpk,cqk->cpq/dot_general | solution.py:202
  90.0 1.4 %convolution_bitcast_fusion = f32[1,8,1,256,256]{4,3,1,2,0:T(8,128)S(1)} fusion(bf16[8,256,128]{2,1,0:T(8,128)(2,1)S(1)} %get-tuple-element.17, bf16[8,256,128]{2,1,0:T(8,128)(2,1)S(1)} %get-tuple-element.16, bf16[8,256,128]{2,1,0:T(8,128)(2,1)S(1)} %get-tuple-element.19, bf16[8,256,128]{2,1,0:T(8,128)(2,1)S(1)} %get-tuple-element.20), kind=kOutput, calls=%fused_computation.31 | convolution fusion | flops 545259520 | bytes 4194304 | tf_op jit(solution)/shard_map/cpk,cqk->cpq/dot_general | solution.py:201
  91.4 0.5 fusion.1
  91.9 0.4 pad_maximum_fusion
  92.3 2.3 %copy.10 = bf16[2,8,2,256,256]{4,3,2,1,0:T(8,128)(2,1)} copy(bf16[2,8,2,256,256]{4,3,1,2,0:T(8,128)(2,1)S(1)} %pad_maximum_fusion) | data formatting | bytes 8388608 | tf_op jit(solution)/shard_map/stack | solution.py:204
  (2 shorter events, 0.1 us)

commit v2 on v1

v2 whole, which is shorter than its diff:
```python
import functools

import jax
import jax.numpy as jnp
import numpy as np
from jax import lax
from jax.sharding import PartitionSpec as P
from jax.experimental import pallas as pl
from jax.experimental.pallas import tpu as pltpu
MESH = pl.DeviceIdType.MESH
FL = dict(relay=True, order=(3, 1, 2, 0), lag=4, xy=True, odd=(0,2), first=((2, 1), (3, 1), (1, 1), (2, 3), (3, 3), (1, 3), (2, 2), (3, 2), (1, 2)), ds=(0,1,2,3), up=6, at=8, last=(1,3,2,0))

def comm_kernel(fl, v, pm, out, s, g, s1, ys, rxy, rz, sx, sz, sr, rf, sf, sg, fin):
    t, c, b = lax.axis_index("tm"), lax.axis_index("chan"), lax.axis_index("bl")
    y, l = lax.div(c, 8), lax.rem(c, 8)

    def piece(cc, bb, half):
        return v.at[:, :, cc, bb, :, pl.ds(half * 128, 128)]

    def spot(o, half, cc):
        return g.at[half, b, cc] if o == 0 else s.at[o - 1, half, cc]

    sem = pltpu.get_barrier_semaphore()
    def greet(**k):
        pl.semaphore_signal(sem, inc=1, device_id=k, device_id_type=MESH)
    for o in (2, 1, 3):
        greet(bl=lax.rem(b + o, 4))
    greet(tm=1 - t)
    far = jnp.where(t == 0, 1, -1)
    greet(tm=1 - t, bl=lax.rem(b - 2 * far + 8, 4))
    greet(tm=1 - t, bl=lax.rem(b - far + 8, 4))
    def greet_xy(i, _):
        greet(chan=lax.rem(c + i, 32))
        return 0
    lax.fori_loop(1, 32, greet_xy, 0)
    for half in (1, 0):
        for o in (2, 3, 1, 0):
            pltpu.make_async_copy(piece(c, lax.rem(b + o, 4), half), spot(o, half, c), rxy.at[o, half, y]).start()
    pl.semaphore_wait(sem, 37)
    if not fl["xy"]:
        for half in (1, 0):
            for o in range(4):
                pltpu.make_async_copy(piece(c, lax.rem(b + o, 4), half), spot(o, half, c), rxy.at[o, half, y]).wait()

    def xysend(half, o, d):
        def send(j, _):
            cc = lax.rem(y + d, 4) * 8 + lax.rem(l + j, 8)
            pltpu.make_async_remote_copy(
                src_ref=piece(cc, lax.rem(b + o, 4), half), dst_ref=spot(o, half, c),
                send_sem=sx.at[o, half], recv_sem=rxy.at[o, half, y],
                device_id={"chan": cc}, device_id_type=MESH).start()
            return 0
        lax.fori_loop(1 if d == 0 else 0, 8, send, 0)

    def rows(ref):
        return ref
    def arrived(ref, sm):
        pltpu.make_async_copy(ref, ref, sm).wait()

    def yg(d):
        return lax.rem(y + 4 - d, 4)
    def eight(d):
        return pl.ds(pl.multiple_of(yg(d) * 8, 8), 8)

    def via_odd(o, d):
        return o == 3 or (o == 2 and d in fl["odd"])

    def zsend(half, o, d):
        part = s.at[o - 1, half, eight(d)]
        if fl["xy"]: arrived(part, rxy.at[o, half, yg(d)])
        if half == 1 and via_odd(o, d) and fl["relay"]:
            to_t = jnp.int32(1)
            h = jnp.where(t == 0, 2, 1)
        else:
            to_t, h = t, half
        pltpu.make_async_remote_copy(
            src_ref=part, dst_ref=g.at[h, b, eight(d)],
            send_sem=sz.at[o, half], recv_sem=rz.at[h, o, yg(d)],
            device_id={"bl": lax.rem(b + o, 4), "tm": to_t}, device_id_type=MESH).start()

    def relay(d, o, h_from, h_to):
        src = lax.rem(b + 4 - o, 4)
        pltpu.make_async_remote_copy(
            src_ref=g.at[h_from, src, eight(d)], dst_ref=g.at[h_to, src, eight(d)],
            send_sem=sr.at[o, d], recv_sem=rz.at[h_to, o, yg(d)],
            device_id={"tm": 1 - t}, device_id_type=MESH).start()

    def landed(h, o, d):
        arrived(g.at[h, lax.rem(b + 4 - o, 4), eight(d)], rz.at[h, o, yg(d)])

    first = fl["first"]
    def far_send(o, d):
        row = pl.multiple_of(lax.rem(y + d, 4) * 8, 8)
        pltpu.make_async_remote_copy(
            src_ref=v.at[:, :, pl.ds(row, 8), lax.rem(b + o, 4), :, pl.ds(0, 128)],
            dst_ref=s1.at[first.index((o, d))],
            send_sem=sf.at[first.index((o, d))], recv_sem=rf.at[first.index((o, d))],
            device_id={"bl": lax.rem(b + o, 4)}, device_id_type=MESH).start()
    def far_pass(o, d):
        k = first.index((o, d))
        arrived(s1.at[k], rf.at[k])
        def send(j, _):
            lane = lax.rem(l + j, 8)
            pltpu.make_async_remote_copy(
                src_ref=s1.at[k, :, :, lane], dst_ref=g.at[0, lax.rem(b + 4 - o, 4), c],
                send_sem=sg.at[k], recv_sem=rz.at[0, o, y],
                device_id={"chan": lax.rem(y + d, 4) * 8 + lane}, device_id_type=MESH).start()
            return 0
        lax.fori_loop(0, 8, send, 0)
    up = fl["up"]
    for u in first[:up]:
        far_send(*u)
    order = fl["order"]
    units = [(half, o, d) for half in (1, 0) for d in fl["ds"] for o in order if half == 1 or (o, d) not in first]
    lag = fl["lag"]
    done = [0]
    def advance(k):
        while done[0] < min(k, len(units)):
            if fl["xy"]: xysend(*units[done[0]])
            done[0] += 1
    def relays(d):
        @pl.when(t == 0)
        def _():
            for o in (1, 2):
                if not via_odd(o, d):
                    landed(1, o, d)
                    relay(d, o, 1, 2)
        @pl.when(t == 1)
        def _():
            for o in (2, 3):
                if via_odd(o, d):
                    landed(2, o, d)
                    relay(d, o, 2, 1)
    for n, u in enumerate(units):
        advance(n + 1 + lag)
        if n == fl["at"]:
            for k in first[up:]:
                far_send(*k)
        half, o, d = u
        if half == 0 and units[n - 1][2] != d or n == 16 and fl["relay"]:
            if n == 16:
                for k in first:
                    far_pass(*k)
            relays(d)
        if o > 0:
            zsend(half, o, d)
        elif half == 1:
            if fl["xy"]: arrived(g.at[1, b, eight(d)], rxy.at[0, 1, yg(d)])
            if fl["relay"]:
                @pl.when(t == 0)
                def _():
                    relay(d, 0, 1, 2)

    def written(h, d):
        at = (h, slice(None), slice(None), pl.ds(pl.multiple_of(yg(d) * 64, 64), 64))
        return pltpu.make_async_copy(ys.at[at], out.at[at], fin.at[h, d])

    def settle(h, d):
        for k in range(2):
            for p in range(2):
                x = g[h, :, pl.ds(yg(d) * 8 + 4 * k, 4), p].reshape(256, 128)
                r = jnp.dot(pm[...], x, preferred_element_type=jnp.float32)
                r = r.astype(jnp.bfloat16).reshape(8, 32, 128)
                ys[h, :, p, pl.ds(pl.multiple_of(yg(d) * 64 + 32 * k, 32), 32), :] = r
        written(h, d).start()

    for d in range(4):
        @pl.when(t == 0)
        def _():
            for o in (2, 3):
                if via_odd(o, d):
                    landed(1, o, d)

        @pl.when(t == 1)
        def _():
            for o in (0, 1, 2):
                if not via_odd(o, d):
                    landed(2, o, d)
            settle(2, d)
            for o in (2, 3, 1):
                landed(1, o, d)
        settle(1, d)
    for d in fl["last"]:
        arrived(g.at[0, b, eight(d)], rxy.at[0, 0, yg(d)])
        for o in (2, 3, 1):
            landed(0, o, d)
        settle(0, d)
    for o in range(4):
        for half in range(2):
            gone = [d for (oo, d) in first if oo == o] if half == 0 else []
            if fl["xy"]: arrived(s.at[0, 0, pl.ds(0, 31 - 8 * len(gone))], sx.at[o, half])
            if o > 0:
                arrived(s.at[0, 0, pl.ds(0, 32 - 8 * len(gone))], sz.at[o, half])
    if fl['relay']:
        for o in range(4):
            for d in range(4):
                @pl.when(t == (1 if via_odd(o, d) else 0))
                def _():
                    arrived(s.at[0, 0, pl.ds(0, 8)], sr.at[o, d])
    for k in range(len(first)):
        arrived(s1.at[k], sf.at[k])
        arrived(s1.at[k], sg.at[k])
    for d in range(4):
        written(1, d).wait()
        written(0, d).wait()

        @pl.when(t == 1)
        def _():
            written(2, d).wait()


def comm(v, pm):
    bf = jnp.bfloat16
    D = pltpu.SemaphoreType.DMA
    return pl.pallas_call(
        functools.partial(comm_kernel, dict(FL)),
        out_shape=jax.ShapeDtypeStruct((3, 8, 2, 256, 128), bf),
        in_specs=[pl.BlockSpec(memory_space=pl.ANY), pl.BlockSpec(memory_space=pltpu.VMEM)],
        out_specs=pl.BlockSpec(memory_space=pl.ANY),
        scratch_shapes=[
            pltpu.VMEM((3, 2, 32, 2, 2, 8, 128), bf),
            pltpu.VMEM((3, 4, 32, 2, 2, 8, 128), bf),
            pltpu.VMEM((max(1, len(FL["first"])), 2, 2, 8, 8, 128), bf),
            pltpu.VMEM((3, 8, 2, 256, 128), bf),
            D((4, 2, 4)), D((3, 4, 4)), D((4, 2)), D((4, 2)), D((4, 4)), D((12,)), D((12,)), D((12,)), D((3, 4)),
        ],
        compiler_params=pltpu.CompilerParams(collective_id=0, has_side_effects=True),
        name="gather",
    )(v.reshape(2, 2, 32, 4, 8, 256), pm)


def corr_kernel(tap, y_ref, o_ref):
    early, late = tap[0:1, :], tap[1:2, :]
    t = lax.axis_index("tm")
    f32, bf = jnp.float32, jnp.bfloat16

    def load(h, p):
        return y_ref[h, 0, p].astype(f32)

    def window(w, lo, ea):
        al, bl_, ae, be = lo[0], lo[1], ea[0], ea[1]
        rhs = jnp.concatenate([al, bl_, ae, be], 1)
        lhs = jnp.concatenate([bl_, -al, be, -ae], 1)
        for i, m in enumerate((rhs, lhs)):
            r = lax.dot_general(m, rhs, (((1,), (1,)), ((), ())), preferred_element_type=f32)
            o_ref[i, 0, w] = (r * (1.0 / 128)).astype(bf)

    a = [load(0, p) for p in (0, 1)]
    tail = [(load(2, p) * early) for p in (0, 1)]
    tail = [jnp.where(t == 1, x, 0.0).astype(bf) for x in tail]
    window(0, [(x * late).astype(bf) for x in a], tail)
    bb = [load(1, p) for p in (0, 1)]
    window(1, [(x * late).astype(bf) for x in bb], [(x * early).astype(bf) for x in a])


def corr(tap, y):
    return pl.pallas_call(
        corr_kernel,
        grid=(8,),
        out_shape=jax.ShapeDtypeStruct((2, 8, 2, 256, 256), jnp.bfloat16),
        in_specs=[
            pl.BlockSpec((2, 128), lambda i: (0, 0)),
            pl.BlockSpec((3, 1, 2, 256, 128), lambda i: (0, i, 0, 0, 0)),
        ],
        out_specs=pl.BlockSpec((2, 1, 2, 256, 256), lambda i: (0, i, 0, 0, 0)),
        compiler_params=pltpu.CompilerParams(dimension_semantics=("arbitrary",)),
        name="corr",
    )(tap, y)


def tapers():
    steps = np.arange(128, dtype=np.float64)
    return np.stack([np.sin(np.pi * (steps + 0.5) / 256), np.sin(np.pi * (steps + 128.5) / 256)]).astype(np.float32)


def perm():
    m = np.zeros((256, 256), np.float32)
    for b in range(4):
        for c in range(4):
            for s in range(2):
                for h in range(8):
                    m[h * 32 + c * 8 + b * 2 + s, ((b * 4 + c) * 2 + s) * 8 + h] = 1
    return m


def local(voltages):
    y = comm(voltages.reshape(2, 2, 128, 8, 256), perm().astype(jnp.bfloat16))
    return corr(tapers(), y)


def solution(mesh):
    return jax.shard_map(
        local,
        mesh=mesh,
        in_specs=(P(None, ("chan", "bl"), None, "tm"),),
        out_specs=P(None, ("chan", "bl"), "tm", None, None),
        check_vma=False,
    )
```

time: 94.6 us -> 78.5 us (0.83)
  the two profiles are of different devices: /device:TPU:33 before, /device:TPU:64 now
where the time goes in v2:
time: 78.5 us; the launch traced here: 78.2 us
  Pallas kernels  78.2 us (100%)
    pallas_call x1, Pallas kernels, comm(): pl.pallas_call(functools.partial(comm_kernel, dict(FL)), out_shape=jax.Sh...  70.2 us
    pallas_call x1, Pallas kernels, corr(): pl.pallas_call(corr_kernel, grid=(8,), out_shape=jax.ShapeDtypeStruct((2,...  8 us

profile of v2, /device:TPU:64, one launch (start us, length us, event | category | flops | bytes accessed | tf_op | source)
XLA Modules:
  0.0 78.2 jit_solution(14332859941291395399)
XLA Ops:
  0.0 70.2 %gather.1.y_ref = bf16[3,8,2,256,128]{4,3,2,1,0:T(8,128)(2,1)} custom-call(bf16[2,2,32,4,8,256]{5,4,3,2,1,0:T(8,128)(2,1)} %bitcast.1, bf16[256,256]{1,0:T(8,128)(2,1)} %constant.4.clone.pm), custom_call_target="tpu_custom_call" | custom-call | tf_op jit(solution)/shard_map/gather/pallas_call | solution.py:215
  70.2 8.0 %corr.1 = bf16[2,8,2,256,256]{4,3,2,1,0:T(8,128)(2,1)} custom-call(f32[2,128]{1,0:T(2,128)} %constant.5.clone.tap, bf16[3,8,2,256,128]{4,3,2,1,0:T(8,128)(2,1)} %gather.1.y_ref), custom_call_target="tpu_custom_call" | custom-call | tf_op jit(solution)/shard_map/corr/pallas_call | solution.py:257

commit v3 on v2

--- a/solution.py
+++ b/solution.py
@@ -10,7 +10,7 @@
 MESH = pl.DeviceIdType.MESH
 FL = dict(relay=True, order=(3, 1, 2, 0), lag=4, xy=True, odd=(0,2), first=((2, 1), (3, 1), (1, 1), (2, 3), (3, 3), (1, 3), (2, 2), (3, 2), (1, 2)), ds=(0,1,2,3), up=6, at=8, last=(1,3,2,0))
 
-def comm_kernel(fl, v, pm, out, s, g, s1, ys, rxy, rz, sx, sz, sr, rf, sf, sg, fin):
+def comm_kernel(fl, v, pm, ys, s, g, s1, rxy, rz, sx, sz, sr, rf, sf, sg):
     t, c, b = lax.axis_index("tm"), lax.axis_index("chan"), lax.axis_index("bl")
     y, l = lax.div(c, 8), lax.rem(c, 8)
 
@@ -151,10 +151,6 @@
                 def _():
                     relay(d, 0, 1, 2)
 
-    def written(h, d):
-        at = (h, slice(None), slice(None), pl.ds(pl.multiple_of(yg(d) * 64, 64), 64))
-        return pltpu.make_async_copy(ys.at[at], out.at[at], fin.at[h, d])
-
     def settle(h, d):
         for k in range(2):
             for p in range(2):
@@ -162,7 +158,6 @@
                 r = jnp.dot(pm[...], x, preferred_element_type=jnp.float32)
                 r = r.astype(jnp.bfloat16).reshape(8, 32, 128)
                 ys[h, :, p, pl.ds(pl.multiple_of(yg(d) * 64 + 32 * k, 32), 32), :] = r
-        written(h, d).start()
 
     for d in range(4):
         @pl.when(t == 0)
@@ -200,13 +195,6 @@
     for k in range(len(first)):
         arrived(s1.at[k], sf.at[k])
         arrived(s1.at[k], sg.at[k])
-    for d in range(4):
-        written(1, d).wait()
-        written(0, d).wait()
-
-        @pl.when(t == 1)
-        def _():
-            written(2, d).wait()
 
 
 def comm(v, pm):
@@ -214,28 +202,36 @@
     D = pltpu.SemaphoreType.DMA
     return pl.pallas_call(
         functools.partial(comm_kernel, dict(FL)),
-        out_shape=jax.ShapeDtypeStruct((3, 8, 2, 256, 128), bf),
+        out_shape=pltpu.VMEM((3, 8, 2, 256, 128), bf),
         in_specs=[pl.BlockSpec(memory_space=pl.ANY), pl.BlockSpec(memory_space=pltpu.VMEM)],
-        out_specs=pl.BlockSpec(memory_space=pl.ANY),
+        out_specs=pl.BlockSpec(memory_space=pltpu.VMEM),
         scratch_shapes=[
             pltpu.VMEM((3, 2, 32, 2, 2, 8, 128), bf),
             pltpu.VMEM((3, 4, 32, 2, 2, 8, 128), bf),
             pltpu.VMEM((max(1, len(FL["first"])), 2, 2, 8, 8, 128), bf),
-            pltpu.VMEM((3, 8, 2, 256, 128), bf),
-            D((4, 2, 4)), D((3, 4, 4)), D((4, 2)), D((4, 2)), D((4, 4)), D((12,)), D((12,)), D((12,)), D((3, 4)),
+            D((4, 2, 4)), D((3, 4, 4)), D((4, 2)), D((4, 2)), D((4, 4)), D((12,)), D((12,)), D((12,)),
         ],
         compiler_params=pltpu.CompilerParams(collective_id=0, has_side_effects=True),
         name="gather",
     )(v.reshape(2, 2, 32, 4, 8, 256), pm)
 
 
+N = 4
+
+
 def corr_kernel(tap, y_ref, o_ref):
+    for n in range(N):
+        one(tap, y_ref, o_ref, n)
+
+
+def one(tap, y_ref, o_ref, n):
+    ch = pl.program_id(0) * N + n
     early, late = tap[0:1, :], tap[1:2, :]
     t = lax.axis_index("tm")
     f32, bf = jnp.float32, jnp.bfloat16
 
     def load(h, p):
-        return y_ref[h, 0, p].astype(f32)
+        return y_ref[h, ch, p].astype(f32)
 
     def window(w, lo, ea):
         al, bl_, ae, be = lo[0], lo[1], ea[0], ea[1]
@@ -243,7 +239,7 @@
         lhs = jnp.concatenate([bl_, -al, be, -ae], 1)
         for i, m in enumerate((rhs, lhs)):
             r = lax.dot_general(m, rhs, (((1,), (1,)), ((), ())), preferred_element_type=f32)
-            o_ref[i, 0, w] = (r * (1.0 / 128)).astype(bf)
+            o_ref[i, n, w] = (r * (1.0 / 128)).astype(bf)
 
     a = [load(0, p) for p in (0, 1)]
     tail = [(load(2, p) * early) for p in (0, 1)]
@@ -256,14 +252,14 @@
 def corr(tap, y):
     return pl.pallas_call(
         corr_kernel,
-        grid=(8,),
+        grid=(8 // N,),
         out_shape=jax.ShapeDtypeStruct((2, 8, 2, 256, 256), jnp.bfloat16),
         in_specs=[
             pl.BlockSpec((2, 128), lambda i: (0, 0)),
-            pl.BlockSpec((3, 1, 2, 256, 128), lambda i: (0, i, 0, 0, 0)),
+            pl.BlockSpec(memory_space=pltpu.VMEM),
         ],
-        out_specs=pl.BlockSpec((2, 1, 2, 256, 256), lambda i: (0, i, 0, 0, 0)),
-        compiler_params=pltpu.CompilerParams(dimension_semantics=("arbitrary",)),
+        out_specs=pl.BlockSpec((2, N, 2, 256, 256), lambda i: (0, i, 0, 0, 0)),
+        compiler_params=pltpu.CompilerParams(dimension_semantics=("arbitrary",), vmem_limit_bytes=24 * 2**20),
         name="corr",
     )(tap, y)
 

time: 78.5 us -> 73.5 us (0.936)
  Pallas kernels: 78.2 us -> 73.4 us
    pallas_call x2, Pallas kernels: 78.2 us -> 73.4 us  [the longest x1 69.5 us: comm(): pl.pallas_call(functools.partial(comm_kernel, dict(FL)), out_shape=pltpu....]
where the time goes in v3:
time: 73.5 us; the launch traced here: 73.4 us
  Pallas kernels  73.4 us (100%)
    pallas_call x1, Pallas kernels, comm(): pl.pallas_call(functools.partial(comm_kernel, dict(FL)), out_shape=pltpu....  69.5 us
    pallas_call x1, Pallas kernels, corr(): pl.pallas_call(corr_kernel, grid=(8 // N,), out_shape=jax.ShapeDtypeStruc...  3.95 us

profile of v3, /device:TPU:64, one launch (start us, length us, event | category | flops | bytes accessed | tf_op | source)
XLA Modules:
  0.0 73.4 jit_solution(11091772002802460501)
XLA Ops:
  0.0 0.0 copy-start
  0.0 69.5 %gather.1.y_ref = bf16[3,8,2,256,128]{4,3,2,1,0:T(8,128)(2,1)S(1)} custom-call(bf16[2,2,32,4,8,256]{5,4,3,2,1,0:T(8,128)(2,1)} %bitcast.1, bf16[256,256]{1,0:T(8,128)(2,1)} %constant.4.clone.pm), custom_call_target="tpu_custom_call" | custom-call | tf_op jit(solution)/shard_map/gather/pallas_call | solution.py:203
  69.5 0.0 copy-done
  69.5 4.0 %corr.1 = bf16[2,8,2,256,256]{4,3,2,1,0:T(8,128)(2,1)} custom-call(f32[2,128]{1,0:T(2,128)S(1)} %copy-done, bf16[3,8,2,256,128]{4,3,2,1,0:T(8,128)(2,1)S(1)} %gather.1.y_ref), custom_call_target="tpu_custom_call" | custom-call | tf_op jit(solution)/shard_map/corr/pallas_call | solution.py:253
Async XLA Ops:
  0.0 69.5 %copy-start = (f32[2,128]{1,0:T(2,128)S(1)}, f32[2,128]{1,0:T(2,128)}, u32[]{:S(2)}) copy-start(f32[2,128]{1,0:T(2,128)} %constant.5.clone.tap) | copy-start | bytes 3076

commit v4 on v3

--- a/solution.py
+++ b/solution.py
@@ -216,16 +216,19 @@
     )(v.reshape(2, 2, 32, 4, 8, 256), pm)
 
 
-N = 4
-
-
-def corr_kernel(tap, y_ref, o_ref):
-    for n in range(N):
+def corr_kernel(tap, y_ref, out, o_ref, sem):
+    def leave(n):
+        return pltpu.make_async_copy(o_ref.at[:, n], out.at[:, n], sem.at[n])
+
+    for n in range(8):
         one(tap, y_ref, o_ref, n)
+        leave(n).start()
+    for n in range(8):
+        leave(n).wait()
 
 
 def one(tap, y_ref, o_ref, n):
-    ch = pl.program_id(0) * N + n
+    ch = n
     early, late = tap[0:1, :], tap[1:2, :]
     t = lax.axis_index("tm")
     f32, bf = jnp.float32, jnp.bfloat16
@@ -252,14 +255,14 @@
 def corr(tap, y):
     return pl.pallas_call(
         corr_kernel,
-        grid=(8 // N,),
         out_shape=jax.ShapeDtypeStruct((2, 8, 2, 256, 256), jnp.bfloat16),
-        in_specs=[
-            pl.BlockSpec((2, 128), lambda i: (0, 0)),
-            pl.BlockSpec(memory_space=pltpu.VMEM),
+        in_specs=[pl.BlockSpec(memory_space=pltpu.VMEM)] * 2,
+        out_specs=pl.BlockSpec(memory_space=pl.ANY),
+        scratch_shapes=[
+            pltpu.VMEM((2, 8, 2, 256, 256), jnp.bfloat16),
+            pltpu.SemaphoreType.DMA((8,)),
         ],
-        out_specs=pl.BlockSpec((2, N, 2, 256, 256), lambda i: (0, i, 0, 0, 0)),
-        compiler_params=pltpu.CompilerParams(dimension_semantics=("arbitrary",), vmem_limit_bytes=24 * 2**20),
+        compiler_params=pltpu.CompilerParams(vmem_limit_bytes=24 * 2**20),
         name="corr",
     )(tap, y)
 

time: 73.5 us -> 72.8 us (level)
  no operation moved by 1% of the time
where the time goes in v4:
time: 72.8 us; the launch traced here: 72.7 us
  Pallas kernels  72.7 us (100%)
    pallas_call x1, Pallas kernels, comm(): pl.pallas_call(functools.partial(comm_kernel, dict(FL)), out_shape=pltpu....  69.5 us
    pallas_call x1, Pallas kernels, corr(): pl.pallas_call(corr_kernel, out_shape=jax.ShapeDtypeStruct((2, 8, 2, 256,...  3.25 us

profile of v4, /device:TPU:64, one launch (start us, length us, event | category | flops | bytes accessed | tf_op | source)
XLA Modules:
  0.0 72.7 jit_solution(3587690869972413337)
XLA Ops:
  0.0 0.0 copy-start
  0.0 69.5 %gather.1.y_ref = bf16[3,8,2,256,128]{4,3,2,1,0:T(8,128)(2,1)S(1)} custom-call(bf16[2,2,32,4,8,256]{5,4,3,2,1,0:T(8,128)(2,1)} %bitcast.1, bf16[256,256]{1,0:T(8,128)(2,1)} %constant.4.clone.pm), custom_call_target="tpu_custom_call" | custom-call | tf_op jit(solution)/shard_map/gather/pallas_call | solution.py:203
  69.5 0.0 copy-done
  69.5 3.3 %corr.1 = bf16[2,8,2,256,256]{4,3,2,1,0:T(8,128)(2,1)} custom-call(f32[2,128]{1,0:T(2,128)S(1)} %copy-done, bf16[3,8,2,256,128]{4,3,2,1,0:T(8,128)(2,1)S(1)} %gather.1.y_ref), custom_call_target="tpu_custom_call" | custom-call | tf_op jit(solution)/shard_map/corr/pallas_call | solution.py:256
Async XLA Ops:
  0.0 69.5 %copy-start = (f32[2,128]{1,0:T(2,128)S(1)}, f32[2,128]{1,0:T(2,128)}, u32[]{:S(2)}) copy-start(f32[2,128]{1,0:T(2,128)} %constant.5.clone.tap) | copy-start | bytes 3076

commit v5 on v4

--- a/solution.py
+++ b/solution.py
@@ -159,6 +159,18 @@
                 r = r.astype(jnp.bfloat16).reshape(8, 32, 128)
                 ys[h, :, p, pl.ds(pl.multiple_of(yg(d) * 64 + 32 * k, 32), 32), :] = r
 
+    @pl.when(t == 1)
+    def _():
+        for d in range(4):
+            for o in (2, 3, 1):
+                landed(1, o, d)
+            settle(1, d)
+
+    for d in fl["last"]:
+        arrived(g.at[0, b, eight(d)], rxy.at[0, 0, yg(d)])
+        for o in (2, 3, 1):
+            landed(0, o, d)
+        settle(0, d)
     for d in range(4):
         @pl.when(t == 0)
         def _():
@@ -171,15 +183,7 @@
             for o in (0, 1, 2):
                 if not via_odd(o, d):
                     landed(2, o, d)
-            settle(2, d)
-            for o in (2, 3, 1):
-                landed(1, o, d)
-        settle(1, d)
-    for d in fl["last"]:
-        arrived(g.at[0, b, eight(d)], rxy.at[0, 0, yg(d)])
-        for o in (2, 3, 1):
-            landed(0, o, d)
-        settle(0, d)
+        settle(1 + t, d)
     for o in range(4):
         for half in range(2):
             gone = [d for (oo, d) in first if oo == o] if half == 0 else []

time: 72.8 us -> 71.7 us (0.985)
  Pallas kernels: 72.7 us -> 71.6 us
    pallas_call x1, Pallas kernels: 69.5 us -> 68.3 us  [comm(): pl.pallas_call(functools.partial(comm_kernel, dict(FL)), out_shape=pltpu....]
where the time goes in v5:
time: 71.7 us; the launch traced here: 71.6 us
  Pallas kernels  71.6 us (100%)
    pallas_call x1, Pallas kernels, comm(): pl.pallas_call(functools.partial(comm_kernel, dict(FL)), out_shape=pltpu....  68.3 us
    pallas_call x1, Pallas kernels, corr(): pl.pallas_call(corr_kernel, out_shape=jax.ShapeDtypeStruct((2, 8, 2, 256,...  3.26 us

profile of v5, /device:TPU:64, one launch (start us, length us, event | category | flops | bytes accessed | tf_op | source)
XLA Modules:
  0.0 71.6 jit_solution(12512483729236726764)
XLA Ops:
  0.0 0.0 copy-start
  0.0 68.3 %gather.1.y_ref = bf16[3,8,2,256,128]{4,3,2,1,0:T(8,128)(2,1)S(1)} custom-call(bf16[2,2,32,4,8,256]{5,4,3,2,1,0:T(8,128)(2,1)} %bitcast.1, bf16[256,256]{1,0:T(8,128)(2,1)} %constant.4.clone.pm), custom_call_target="tpu_custom_call" | custom-call | tf_op jit(solution)/shard_map/gather/pallas_call | solution.py:207
  68.3 0.0 copy-done
  68.3 3.3 %corr.1 = bf16[2,8,2,256,256]{4,3,2,1,0:T(8,128)(2,1)} custom-call(f32[2,128]{1,0:T(2,128)S(1)} %copy-done, bf16[3,8,2,256,128]{4,3,2,1,0:T(8,128)(2,1)S(1)} %gather.1.y_ref), custom_call_target="tpu_custom_call" | custom-call | tf_op jit(solution)/shard_map/corr/pallas_call | solution.py:260
Async XLA Ops:
  0.0 68.3 %copy-start = (f32[2,128]{1,0:T(2,128)S(1)}, f32[2,128]{1,0:T(2,128)}, u32[]{:S(2)}) copy-start(f32[2,128]{1,0:T(2,128)} %constant.5.clone.tap) | copy-start | bytes 3076
